TPU v7x, 32 devices: a whole 2x2x4 slice. The times are simulated.
32 devices in a mesh: depth: 4 (over y, core), blk: 8 (over z, x).
Axes of the slice: x: 2, y: 2, z: 4, core: 2. Of those that a mesh axis runs over, the one named last changes fastest.
Arguments:
- jacobian: bfloat16 [96, 16384], P(('depth', 'blk')), may hold values from -6 to 6
- gain_inverse: bfloat16 [16384, 16384], P('depth', 'blk'), may hold values from -0.00024414062 to 0.00048828125, as said below
- variance: float32 [96], P(('depth', 'blk')), may hold values from 2 to 12
Outputs:
- omega_diag: float32 [96], P(('depth', 'blk'))
Inputs may be any that keep to these rules, and one draw needn't show every extreme that they name: gain_inverse is symmetric and positive definite.
All inputs are finite; a program needn't handle non-finite values.
Results may differ from a plain program's by a relative error of at most 0.0003.
Values may be sent and summed in bfloat16 or wider, within the bound.
A program may use at most 128 MiB of HBM per device.

v0:
```python
import jax
import jax.numpy as jnp
from jax import lax
from jax.sharding import PartitionSpec as P


def shards(jacobian, gain_inverse, variance):
    rows_local = jacobian.shape[0]
    depth_count = lax.axis_size("depth")
    blk_count = lax.axis_size("blk")
    quarter_rows = lax.all_to_all(jacobian, "depth", split_axis=1, concat_axis=0, tiled=True)
    whole_rows = lax.all_gather(jacobian, "depth", axis=0, tiled=True)
    panel = lax.all_to_all(whole_rows, "blk", split_axis=1, concat_axis=0, tiled=True)
    projected = jnp.dot(
        lax.all_gather(quarter_rows, "blk", axis=0, tiled=True),
        gain_inverse,
        preferred_element_type=jnp.float32,
    )
    partial_sum = jnp.sum(projected * panel.astype(jnp.float32), axis=1)
    by_section = partial_sum.reshape(blk_count, depth_count * rows_local)
    reduced = lax.psum_scatter(by_section, "blk", scatter_dimension=0, tiled=True).reshape(-1)
    quadratic = lax.psum_scatter(reduced, "depth", scatter_dimension=0, tiled=True)
    return variance - quadratic


def solution(mesh):
    in_specs = (P(("depth", "blk"), None), P("depth", "blk"), P(("depth", "blk")))
    out_specs = P(("depth", "blk"))
    return jax.shard_map(shards, mesh=mesh, in_specs=in_specs, out_specs=out_specs, check_vma=False)
```

profile of v0, /device:TPU:0, one launch (start us, length us, event | category | flops | bytes accessed | tf_op | source)
XLA Modules:
  0.0 96.0 jit_solution(18339546582499330617)
XLA Ops:
  0.0 4.3 %all-to-all-start = ((bf16[3,4,4096]{2,0,1:T(4,128)(2,1)}), bf16[3,4,4096]{2,0,1:T(4,128)(2,1)S(1)}, u32[]{:S(2)}, u32[]{:S(2)}) async-start(bf16[3,4,4096]{2,0,1:T(4,128)(2,1)} %bitcast.11), calls=%async_computation | async-start | bytes 262144 | tf_op jit(solution)/shard_map/all_to_all | solution.py:11
  4.3 8.3 %all-gather.1 = bf16[4,3,16384]{2,1,0:T(4,128)(2,1)S(1)} all-gather(bf16[1,3,16384]{2,1,0:T(4,128)(2,1)} %bitcast.12), channel_id=1, replica_groups=mesh['depth'=4,'blk'=8] {'depth'}, dimensions={0}, use_global_device_ids=true | all-gather | bytes 491520 | tf_op jit(solution)/shard_map/all_gather | solution.py:12
  12.5 0.5 all_to_all.28
  13.1 0.0 copy-start
  13.1 1.0 %copy.8 = bf16[12,8,2048]{2,0,1:T(8,128)(2,1)} copy(bf16[12,8,2048]{2,1,0:T(8,128)(2,1)S(1)} %all_to_all.28) | data formatting | bytes 786432 | tf_op jit(solution)/shard_map/all_to_all | solution.py:13
  14.1 0.0 all-to-all-done
  14.1 6.3 %all-to-all-start.1 = ((bf16[12,8,2048]{2,0,1:T(8,128)(2,1)}), bf16[12,8,2048]{2,0,1:T(8,128)(2,1)S(1)}, u32[]{:S(2)}, u32[]{:S(2)}) async-start(bf16[12,8,2048]{2,0,1:T(8,128)(2,1)} %copy.8), calls=%async_computation.1 | async-start | bytes 1048576 | tf_op jit(solution)/shard_map/all_to_all | solution.py:13
  20.4 1.2 %dynamic-slice = u32[1]{0:T(128)} dynamic-slice(u32[32]{0:T(128)} %constant.6, u32[]{:T(128)S(6)} %add.5), dynamic_slice_sizes={1} | dynamic-slice | bytes 12
  21.7 1.3 %dynamic-slice.2 = u32[1]{0:T(128)} dynamic-slice(u32[32]{0:T(128)} %constant.10, u32[]{:T(128)S(6)} %add.5), dynamic_slice_sizes={1} | dynamic-slice | bytes 12
  23.0 0.1 reshape.17
  23.1 37.9 %all-gather = bf16[8,12,4096]{2,1,0:T(8,128)(2,1)S(1)} all-gather(bf16[1,12,4096]{2,1,0:T(8,128)(2,1)S(1)} %reshape.17), channel_id=1, replica_groups=mesh['depth'=4,'blk'=8] {'blk'}, dimensions={0}, use_global_device_ids=true | all-gather | bytes 884736 | tf_op jit(solution)/shard_map/all_gather | solution.py:15
  61.0 0.2 reshape.18
  61.1 0.0 all-to-all-done.1
  61.2 0.1 convert_bitcast_fusion
  61.3 0.1 reshape.16
  61.4 8.7 %fusion = f32[96]{0:T(128)S(1)} fusion(f32[96,2048]{1,0:T(8,128)S(1)} %reshape.16, bf16[96,4096]{1,0:T(8,128)(2,1)S(1)} %reshape.18, bf16[4096,2048]{1,0:T(8,128)(2,1)} %param.4), kind=kOutput, calls=%fused_computation.1 | convolution fusion | flops 1611005824 | bytes 18350464 | tf_op jit(solution)/shard_map/dot_general | solution.py:14
  70.0 0.1 reshape.14
  70.1 18.3 %all-reduce = f32[8,12]{1,0:T(8,128)S(1)} all-reduce(f32[8,12]{1,0:T(8,128)S(1)} %reshape.14), channel_id=2, replica_groups=mesh['depth'=4,'blk'=8] {'blk'}, use_global_device_ids=true, to_apply=%region_1.0.clone | all-reduce | flops 96 | bytes 768
  88.4 0.6 dynamic-slice_bitcast_fusion
  89.7 5.7 %all-reduce.1 = f32[12]{0:T(128)S(1)} all-reduce(f32[12]{0:T(128)S(1)} %dynamic-slice_bitcast_fusion), channel_id=3, replica_groups=mesh['depth'=4,'blk'=8] {'depth'}, use_global_device_ids=true, to_apply=%region_2.0.clone | all-reduce | flops 12 | bytes 96
  95.4 0.0 copy-done
  95.4 0.6 dynamic-slice_subtract_fusion
Async XLA Ops:
  0.0 14.1 %all-to-all-start = ((bf16[3,4,4096]{2,0,1:T(4,128)(2,1)}), bf16[3,4,4096]{2,0,1:T(4,128)(2,1)S(1)}, u32[]{:S(2)}, u32[]{:S(2)}) async-start(bf16[3,4,4096]{2,0,1:T(4,128)(2,1)} %bitcast.11), calls=%async_computation | async-start | bytes 262144 | tf_op jit(solution)/shard_map/all_to_all | solution.py:11
  13.1 82.3 %copy-start = (f32[3]{0:T(128)S(1)}, f32[3]{0:T(128)}, u32[]{:S(2)}) copy-start(f32[3]{0:T(128)} %param.5) | copy-start | bytes 40
  14.1 47.0 %all-to-all-start.1 = ((bf16[12,8,2048]{2,0,1:T(8,128)(2,1)}), bf16[12,8,2048]{2,0,1:T(8,128)(2,1)S(1)}, u32[]{:S(2)}, u32[]{:S(2)}) async-start(bf16[12,8,2048]{2,0,1:T(8,128)(2,1)} %copy.8), calls=%async_computation.1 | async-start | bytes 1048576 | tf_op jit(solution)/shard_map/all_to_all | solution.py:13
where the time goes:
time: 96.4 us; the launch traced here: 96 us
  blocking collectives  70.1 us (73%)
  starting transfers between devices  10.6 us (11%)
  matrix products  8.66 us (9%)
  local copies, waits for them, and re-layouts  5.19 us (5%)
    all_gather x1, blocking collectives, shards(): lax.all_gather(quarter_rows, 'blk', axis=0, tiled=True)  37.9 us
    unnamed x2, blocking collectives  24 us
    dot_general x1, matrix products, shards(): jnp.dot(lax.all_gather(quarter_rows, 'blk', axis=0, tiled=True), gain_inv...  8.66 us
    all_gather x1, blocking collectives, shards(): whole_rows = lax.all_gather(jacobian, 'depth', axis=0, tiled=True)  8.27 us
    all_to_all x1, starting transfers between devices, shards(): lax.all_to_all(whole_rows, 'blk', split_axis=1, concat_axis=0, tiled=True)  6.31 us
    all_to_all x1, starting transfers between devices, shards(): lax.all_to_all(jacobian, 'depth', split_axis=1, concat_axis=0, tiled=True)  4.26 us
    unnamed x6, local copies, waits for them, and re-layouts  2.82 us
  transfers between devices with their start and end apart: 2, of which 0 were waited for; matrix products, arithmetic and copies ran while one was open for 4% of the time, Pallas kernels for 0%

commit v1 on v0

--- a/solution.py
+++ b/solution.py
@@ -12,7 +12,9 @@
     whole_rows = lax.all_gather(jacobian, "depth", axis=0, tiled=True)
     panel = lax.all_to_all(whole_rows, "blk", split_axis=1, concat_axis=0, tiled=True)
     projected = jnp.dot(
-        lax.all_gather(quarter_rows, "blk", axis=0, tiled=True),
+        jnp.concatenate(
+            lax.all_to_all(jnp.stack([quarter_rows] * lax.axis_size("blk")), "blk", 0, 0), axis=0
+        ),
         gain_inverse,
         preferred_element_type=jnp.float32,
     )

time: 96.4 us -> 103 us (1.068)
  waiting for transfers between devices: 0.01 us -> 38.1 us
  blocking collectives: 70.1 us -> 33.4 us
  starting transfers between devices: 10.6 us -> 14.2 us
  local copies, waits for them, and re-layouts: 5.19 us -> 6.28 us
    all_gather x1 -> x0, blocking collectives: 37.9 us -> none  [shards(): lax.all_gather(quarter_rows, 'blk', axis=0, tiled=True)]
    all_to_all x0 -> x1, waiting for transfers between devices: none -> 23.2 us  [shards(): lax.all_to_all(jnp.stack([quarter_rows] * lax.axis_size('blk')), 'blk', 0...]
    all_to_all x1, waiting for transfers between devices: 0.01 us -> 14.9 us  [shards(): lax.all_to_all(whole_rows, 'blk', split_axis=1, concat_axis=0, tiled=True)]
    all_to_all x0 -> x1, starting transfers between devices: none -> 3.64 us  [shards(): lax.all_to_all(jnp.stack([quarter_rows] * lax.axis_size('blk')), 'blk', 0...]
    another operation x0 -> x2, local copies, waits for them, and re-layouts: none -> 1.18 us  [shards(): jnp.stack([quarter_rows] * lax.axis_size('blk'))]
    unnamed x2, blocking collectives: 24 us -> 25.1 us
    unnamed x6 -> x4, local copies, waits for them, and re-layouts: 2.82 us -> 2.56 us
  transfers between devices with their start and end apart: 2 -> 3, of which waited for: 0 -> 2; matrix products, arithmetic and copies ran while one was open for 4% -> 4% of each run, Pallas kernels for 0% -> 0%
where the time goes in v1:
time: 103 us; the launch traced here: 102 us
  waiting for transfers between devices  38.1 us (37%)
  blocking collectives  33.4 us (32%)
  starting transfers between devices  14.2 us (14%)
  matrix products  8.67 us (8%)
  local copies, waits for them, and re-layouts  6.28 us (6%)
    unnamed x2, blocking collectives  25.1 us
    all_to_all x1, waiting for transfers between devices, shards(): lax.all_to_all(jnp.stack([quarter_rows] * lax.axis_size('blk')), 'blk', 0...  23.2 us
    all_to_all x1, waiting for transfers between devices, shards(): lax.all_to_all(whole_rows, 'blk', split_axis=1, concat_axis=0, tiled=True)  14.9 us
    dot_general x1, matrix products, shards(): jnp.dot(jnp.concatenate(lax.all_to_all(jnp.stack([quarter_rows] * lax.axi...  8.67 us
    all_gather x1, blocking collectives, shards(): whole_rows = lax.all_gather(jacobian, 'depth', axis=0, tiled=True)  8.27 us
    all_to_all x1, starting transfers between devices, shards(): lax.all_to_all(whole_rows, 'blk', split_axis=1, concat_axis=0, tiled=True)  6.31 us
    all_to_all x1, starting transfers between devices, shards(): lax.all_to_all(jacobian, 'depth', split_axis=1, concat_axis=0, tiled=True)  4.26 us
    all_to_all x1, starting transfers between devices, shards(): lax.all_to_all(jnp.stack([quarter_rows] * lax.axis_size('blk')), 'blk', 0...  3.64 us
  transfers between devices with their start and end apart: 3, of which 2 were waited for; matrix products, arithmetic and copies ran while one was open for 4% of the time, Pallas kernels for 0%

profile of v1, /device:TPU:0, one launch (start us, length us, event | category | flops | bytes accessed | tf_op | source)
XLA Modules:
  0.0 102.1 jit_solution(16660779259502395894)
XLA Ops:
  0.0 4.3 %all-to-all-start = ((bf16[3,4,4096]{2,0,1:T(4,128)(2,1)}), bf16[3,4,4096]{2,0,1:T(4,128)(2,1)S(1)}, u32[]{:S(2)}, u32[]{:S(2)}) async-start(bf16[3,4,4096]{2,0,1:T(4,128)(2,1)} %bitcast.11), calls=%async_computation | async-start | bytes 262144 | tf_op jit(solution)/shard_map/all_to_all | solution.py:11
  4.3 8.3 %all-gather = bf16[4,3,16384]{2,1,0:T(4,128)(2,1)S(1)} all-gather(bf16[1,3,16384]{2,1,0:T(4,128)(2,1)} %bitcast.12), channel_id=1, replica_groups=mesh['depth'=4,'blk'=8] {'depth'}, dimensions={0}, use_global_device_ids=true | all-gather | bytes 491520 | tf_op jit(solution)/shard_map/all_gather | solution.py:12
  12.5 0.5 all_to_all.29
  13.1 1.0 %copy.8 = bf16[12,8,2048]{2,0,1:T(8,128)(2,1)} copy(bf16[12,8,2048]{2,1,0:T(8,128)(2,1)S(1)} %all_to_all.29) | data formatting | bytes 786432 | tf_op jit(solution)/shard_map/all_to_all | solution.py:13
  14.1 0.0 all-to-all-done
  14.1 6.3 %all-to-all-start.2 = ((bf16[12,8,2048]{2,0,1:T(8,128)(2,1)}), bf16[12,8,2048]{2,0,1:T(8,128)(2,1)S(1)}, u32[]{:S(2)}, u32[]{:S(2)}) async-start(bf16[12,8,2048]{2,0,1:T(8,128)(2,1)} %copy.8), calls=%async_computation.2 | async-start | bytes 1048576 | tf_op jit(solution)/shard_map/all_to_all | solution.py:13
  20.4 0.1 stack.4
  20.5 0.0 copy-start
  20.5 14.9 %all-to-all-done.2 = bf16[12,8,2048]{2,0,1:T(8,128)(2,1)S(1)} async-done(((bf16[12,8,2048]{2,0,1:T(8,128)(2,1)}), bf16[12,8,2048]{2,0,1:T(8,128)(2,1)S(1)}, u32[]{:S(2)}, u32[]{:S(2)}) %all-to-all-start.2) | async-done | bytes 393248 | tf_op jit(solution)/shard_map/all_to_all | solution.py:13
  35.4 1.1 %stack.5 = bf16[8,12,4096]{2,1,0:T(8,128)(2,1)} broadcast(bf16[12,4096]{1,0:T(8,128)(2,1)S(1)} %stack.4), dimensions={1,2} | broadcast | bytes 884736 | tf_op jit(solution)/shard_map/stack | solution.py:16
  36.5 3.6 %all-to-all-start.1 = ((bf16[8,12,4096]{2,1,0:T(8,128)(2,1)}), bf16[8,12,4096]{2,1,0:T(8,128)(2,1)S(1)}, u32[]{:S(2)}, u32[]{:S(2)}) async-start(bf16[8,12,4096]{2,1,0:T(8,128)(2,1)} %stack.5), calls=%async_computation.1 | async-start | bytes 2097152 | tf_op jit(solution)/shard_map/all_to_all | solution.py:16
  40.1 1.2 %dynamic-slice = u32[1]{0:T(128)} dynamic-slice(u32[32]{0:T(128)} %constant.6, u32[]{:T(128)S(6)} %add.5), dynamic_slice_sizes={1} | dynamic-slice | bytes 12
  41.4 1.3 %dynamic-slice.2 = u32[1]{0:T(128)} dynamic-slice(u32[32]{0:T(128)} %constant.10, u32[]{:T(128)S(6)} %add.5), dynamic_slice_sizes={1} | dynamic-slice | bytes 12
  42.7 0.1 convert_bitcast_fusion
  42.8 0.1 reshape.23
  42.9 23.2 %all-to-all-done.1 = bf16[8,12,4096]{2,1,0:T(8,128)(2,1)S(1)} async-done(((bf16[8,12,4096]{2,1,0:T(8,128)(2,1)}), bf16[8,12,4096]{2,1,0:T(8,128)(2,1)S(1)}, u32[]{:S(2)}, u32[]{:S(2)}) %all-to-all-start.1) | async-done | bytes 786464 | tf_op jit(solution)/shard_map/all_to_all | solution.py:16
  66.1 0.2 reshape.20
  66.3 8.7 %fusion = f32[96]{0:T(128)S(1)} fusion(f32[96,2048]{1,0:T(8,128)S(1)} %reshape.23, bf16[96,4096]{1,0:T(8,128)(2,1)S(1)} %reshape.20, bf16[4096,2048]{1,0:T(8,128)(2,1)} %param.4), kind=kOutput, calls=%fused_computation.1 | convolution fusion | flops 1611005824 | bytes 18350464 | tf_op jit(solution)/shard_map/dot_general | solution.py:14
  75.0 0.1 reshape.21
  75.0 19.5 %all-reduce = f32[8,12]{1,0:T(8,128)S(1)} all-reduce(f32[8,12]{1,0:T(8,128)S(1)} %reshape.21), channel_id=2, replica_groups=mesh['depth'=4,'blk'=8] {'blk'}, use_global_device_ids=true, to_apply=%region_1.0.clone | all-reduce | flops 96 | bytes 768
  94.5 0.6 dynamic-slice_bitcast_fusion
  95.8 5.7 %all-reduce.1 = f32[12]{0:T(128)S(1)} all-reduce(f32[12]{0:T(128)S(1)} %dynamic-slice_bitcast_fusion), channel_id=3, replica_groups=mesh['depth'=4,'blk'=8] {'depth'}, use_global_device_ids=true, to_apply=%region_2.0.clone | all-reduce | flops 12 | bytes 96
  101.5 0.0 copy-done
  101.5 0.6 dynamic-slice_subtract_fusion
Async XLA Ops:
  0.0 14.1 %all-to-all-start = ((bf16[3,4,4096]{2,0,1:T(4,128)(2,1)}), bf16[3,4,4096]{2,0,1:T(4,128)(2,1)S(1)}, u32[]{:S(2)}, u32[]{:S(2)}) async-start(bf16[3,4,4096]{2,0,1:T(4,128)(2,1)} %bitcast.11), calls=%async_computation | async-start | bytes 262144 | tf_op jit(solution)/shard_map/all_to_all | solution.py:11
  14.1 21.3 %all-to-all-start.2 = ((bf16[12,8,2048]{2,0,1:T(8,128)(2,1)}), bf16[12,8,2048]{2,0,1:T(8,128)(2,1)S(1)}, u32[]{:S(2)}, u32[]{:S(2)}) async-start(bf16[12,8,2048]{2,0,1:T(8,128)(2,1)} %copy.8), calls=%async_computation.2 | async-start | bytes 1048576 | tf_op jit(solution)/shard_map/all_to_all | solution.py:13
  20.5 81.0 %copy-start = (f32[3]{0:T(128)S(1)}, f32[3]{0:T(128)}, u32[]{:S(2)}) copy-start(f32[3]{0:T(128)} %param.5) | copy-start | bytes 40
  36.5 29.6 %all-to-all-start.1 = ((bf16[8,12,4096]{2,1,0:T(8,128)(2,1)}), bf16[8,12,4096]{2,1,0:T(8,128)(2,1)S(1)}, u32[]{:S(2)}, u32[]{:S(2)}) async-start(bf16[8,12,4096]{2,1,0:T(8,128)(2,1)} %stack.5), calls=%async_computation.1 | async-start | bytes 2097152 | tf_op jit(solution)/shard_map/all_to_all | solution.py:16
